TPU v7x, 32 devices: a whole 2x2x4 slice. The times are simulated.
32 devices in a mesh: gx: 16 (over z, y, core), gy: 2 (over x).
Axes of the slice: x: 2, y: 2, z: 4, core: 2. Of those that a mesh axis runs over, the one named last changes fastest.
Arguments:
- right_side: float32 [16, 2, 512, 256], P('gx', 'gy'), may hold values from -8 to 8, as said below
- coords: float32 [16, 2, 2, 512], P('gx', 'gy'), may hold values from 0 to 1
- noise: float32 [16, 2, 512], P('gx', 'gy'), may hold values from 0.25 to 1
- intersect: int32 [16, 2, 128], P('gx', 'gy'), may hold values from 0 to 4607, as said below
Outputs:
- solution: float32 [16, 2, 512, 256], P('gx', 'gy')
- residual: float32 [16, 2, 512, 256], P('gx', 'gy')
Inputs may be any that keep to these rules, and one draw needn't show every extreme that they name: `right_side`: right-hand sides of order one. `intersect`: each subdomain's list holds 128 distinct indices in increasing order; none names the subdomain itself (block number 4) or a subdomain beyond the first or last one along the second dimension.
All inputs are finite; a program needn't handle non-finite values.
Results may differ from a plain program's by a relative error of at most 0.0003.
Values sent between devices are 32-bit elements; how exact they have to be, the bound alone decides.
A program may use at most 128 MiB of HBM per device.

v0:
```python
import math

import jax
import jax.numpy as jnp
from jax import lax
from jax.sharding import PartitionSpec as P

ITERS = 3


RANGE_LEN = 0.25
ROOT_THREE = math.sqrt(3.0)
HIGH = lax.Precision.HIGHEST


def shifted(value, axis, by):
    count = lax.axis_size(axis)
    return lax.ppermute(value, axis, [(i, (i + by) % count) for i in range(count)])


def passed_along(block, axis, distance):
    devices = range(lax.axis_size(axis))
    route = [(i - distance, i) for i in devices if i - distance in devices]
    return lax.ppermute(block, axis, route)


def kernel_block(rows_pos, cols_pos):
    delta_x = rows_pos[0][:, None] - cols_pos[0][None, :]
    delta_y = rows_pos[1][:, None] - cols_pos[1][None, :]
    distance = jnp.sqrt(delta_x * delta_x + delta_y * delta_y)
    scaled = ROOT_THREE / RANGE_LEN * distance
    clipped = jnp.minimum(distance, 1.0)
    taper_val = jnp.square(jnp.square(1.0 - clipped)) * (4.0 * clipped + 1.0)
    return (1.0 + scaled) * jnp.exp(-scaled) * taper_val


def window_values(values):
    beside = {}
    for step_by in (1, -1):
        beside[step_by] = shifted(values, "gx", step_by)
    column = jnp.stack([beside[1], values, beside[-1]])
    across = {}
    for step_by in (1, -1):
        across[step_by] = passed_along(column, "gy", step_by)
    return [across[1], column, across[-1]]


def window_index(values):
    beside = {}
    for step_by in (1, -1):
        beside[step_by] = shifted(values, "gx", step_by)
    column = jnp.stack([beside[1], values, beside[-1]])
    across = {}
    for step_by in (1, -1):
        across[step_by] = passed_along(column, "gy", step_by)
    return [across[1], column, across[-1]]


def column_sum(first, second):
    return jnp.sum(first * second, axis=0)


def residual_dot(residue, precond):
    return lax.psum(column_sum(residue, precond), ("gx", "gy"))


def shards(right_side, coords, noise, intersect):
    points = right_side.shape[2]
    rhs_count = right_side.shape[3]
    intersect_len = intersect.shape[2]
    ext_len = points + intersect_len
    own_pos = coords.reshape(2, points)
    own_noise = noise.reshape(points)
    point_info = jnp.concatenate([own_pos, own_noise[None, :]], axis=0)
    info_cols = window_values(point_info)
    positions = [
        [
            jnp.stack(
                [
                    info_cols[col_off][row_off, 0] + float(row_off - 1),
                    info_cols[col_off][row_off, 1] + float(col_off - 1),
                ]
            )
            for col_off in range(3)
        ]
        for row_off in range(3)
    ]
    intersect_ids = intersect.reshape(intersect_len)
    block_id = intersect_ids // points
    row_in = intersect_ids % points
    row_of = block_id // 3
    col_of = block_id % 3
    local_id = row_of * points + row_in
    picked_info = [
        jnp.take(
            jnp.transpose(info_cols[col_off], (1, 0, 2)).reshape(3, 3 * points), local_id, axis=1
        )
        for col_off in range(3)
    ]
    chosen = jnp.where(
        col_of[None, :] == 0,
        picked_info[0],
        jnp.where(col_of[None, :] == 1, picked_info[1], picked_info[2]),
    )
    ov_pos = jnp.stack(
        [chosen[0] + (row_of - 1).astype(jnp.float32), chosen[1] + (col_of - 1).astype(jnp.float32)]
    )
    ext_pos = jnp.concatenate([own_pos, ov_pos], axis=1)
    ext_noise = jnp.concatenate([own_noise, chosen[2]])
    local_matrix = kernel_block(ext_pos, ext_pos) + jnp.diag(ext_noise)
    factor = jnp.linalg.cholesky(local_matrix)
    inv_factor = lax.linalg.triangular_solve(
        factor, jnp.eye(ext_len, dtype=jnp.float32), left_side=True, lower=True
    )
    inverse = jnp.dot(inv_factor.T, inv_factor, precision=HIGH, preferred_element_type=jnp.float32)
    near_ids = window_index(intersect_ids)
    point_iota = jnp.arange(points, dtype=jnp.int32)[:, None]
    row_base = (2 - jnp.arange(3, dtype=jnp.int32))[:, None] * 3
    selectors = []
    for col_off in range(3):
        own_rows = near_ids[col_off] - (row_base + (2 - col_off)) * points
        selectors.append((point_iota == own_rows.reshape(1, 3 * intersect_len)).astype(jnp.float32))

    def borrowed_rows(residue):
        requested = [
            lax.dot_general(
                selectors[col_off],
                residue,
                (((0,), (0,)), ((), ())),
                precision=HIGH,
                preferred_element_type=jnp.float32,
            ).reshape(3, intersect_len, rhs_count)
            for col_off in range(3)
        ]
        combined = jnp.stack([requested[col_off][1] for col_off in range(3)])
        for step_by, row_off in ((-1, 0), (1, 2)):
            outgoing = jnp.stack([requested[col_off][row_off] for col_off in range(3)])
            combined = combined + shifted(outgoing, "gx", step_by)
        gathered = combined[1]
        for step_by, col_off in ((-1, 0), (1, 2)):
            gathered = gathered + passed_along(combined[col_off], "gy", step_by)
        return gathered

    def precondition(residue):
        gathered = borrowed_rows(residue)
        extended = jnp.concatenate([residue, gathered], axis=0)
        solved = jnp.dot(inverse, extended, precision=HIGH, preferred_element_type=jnp.float32)
        returned = window_values(solved[points:])
        result = solved[:points]
        for col_off in range(3):
            result = result + jnp.dot(
                selectors[col_off],
                returned[col_off].reshape(3 * intersect_len, rhs_count),
                precision=HIGH,
                preferred_element_type=jnp.float32,
            )
        return result

    noise_col = own_noise[:, None]
    residual = right_side.reshape(points, rhs_count)
    solution = jnp.zeros_like(residual)
    precond = precondition(residual)
    direction = precond
    inner_now = residual_dot(residual, precond)
    for iteration in range(ITERS):
        columns = window_values(direction)
        accumulated = noise_col * direction
        for operate_row_off in range(3):
            for operate_col_off in range(3):
                accumulated = accumulated + jnp.dot(
                    kernel_block(own_pos, positions[operate_row_off][operate_col_off]),
                    columns[operate_col_off][operate_row_off],
                    precision=HIGH,
                    preferred_element_type=jnp.float32,
                )
        step_size = inner_now / lax.psum(column_sum(direction, accumulated), ("gx", "gy"))
        solution = solution + step_size * direction
        residual = residual - step_size * accumulated
        if iteration + 1 < ITERS:
            precond = precondition(residual)
            inner_next = residual_dot(residual, precond)
            direction = precond + inner_next / inner_now * direction
            inner_now = inner_next
    return (solution.reshape(1, 1, points, rhs_count), residual.reshape(1, 1, points, rhs_count))


def solution(mesh):
    placed = (
        P("gx", "gy", None, None),
        P("gx", "gy", None, None),
        P("gx", "gy", None),
        P("gx", "gy", None),
    )
    return jax.shard_map(
        shards,
        mesh=mesh,
        in_specs=placed,
        out_specs=(P("gx", "gy", None, None), P("gx", "gy", None, None)),
        check_vma=False,
    )
```

profile of v0, /device:TPU:0, one launch (start us, length us, event | category | flops | bytes accessed | tf_op | source)
XLA Modules:
  0.0 750.6 jit_solution(9324209336027450057)
XLA Ops:
  1.2 5.0 collective-permute-start.5
  7.0 4.4 collective-permute-start.1
  15.4 4.5 collective-permute-start.6
  23.5 3.7 collective-permute-start.2
  34.4 3.1 add_multiply_fusion
  38.7 11.7 %cholesky.132 = f32[128,128]{1,0:T(8,128)S(1)} custom-call(f32[128,128]{1,0:T(8,128)S(1)} %cholesky.337), custom_call_target="Cholesky" | custom-call | tf_op jit(solution)/shard_map/jit(cholesky)/cholesky | solution.py:111
  50.6 9.8 %custom-call.38 = f32[1,128,128]{1,2,0:T(8,128)S(1)} custom-call(f32[1,128,128]{2,1,0:T(8,128)S(1)} %get-tuple-element.83), custom_call_target="InvertDiagBlocksLowerTriangular" | custom-call | tf_op jit(solution)/shard_map/jit(cholesky)/cholesky | solution.py:111
  63.1 11.9 %cholesky.270 = f32[128,128]{1,0:T(8,128)S(1)} custom-call(f32[128,128]{1,0:T(8,128)S(1)} %cholesky.341), custom_call_target="Cholesky" | custom-call | tf_op jit(solution)/shard_map/jit(cholesky)/cholesky | solution.py:111
  76.3 9.8 %custom-call.39 = f32[1,128,128]{1,2,0:T(8,128)S(1)} custom-call(f32[1,128,128]{2,1,0:T(8,128)S(1)} %get-tuple-element.80), custom_call_target="InvertDiagBlocksLowerTriangular" | custom-call | tf_op jit(solution)/shard_map/jit(cholesky)/cholesky | solution.py:111
  87.8 11.7 %cholesky.291 = f32[128,128]{1,0:T(8,128)S(1)} custom-call(f32[128,128]{1,0:T(8,128)S(1)} %cholesky.346), custom_call_target="Cholesky" | custom-call | tf_op jit(solution)/shard_map/jit(cholesky)/cholesky | solution.py:111
  100.3 9.8 %custom-call.40 = f32[1,128,128]{1,2,0:T(8,128)S(1)} custom-call(f32[1,128,128]{2,1,0:T(8,128)S(1)} %get-tuple-element.77), custom_call_target="InvertDiagBlocksLowerTriangular" | custom-call | tf_op jit(solution)/shard_map/jit(cholesky)/cholesky | solution.py:111
  112.0 11.7 %cholesky.310 = f32[128,128]{1,0:T(8,128)S(1)} custom-call(f32[128,128]{1,0:T(8,128)S(1)} %cholesky.351), custom_call_target="Cholesky" | custom-call | tf_op jit(solution)/shard_map/jit(cholesky)/cholesky | solution.py:111
  124.4 9.8 %custom-call.41 = f32[1,128,128]{1,2,0:T(8,128)S(1)} custom-call(f32[1,128,128]{2,1,0:T(8,128)S(1)} %get-tuple-element.74), custom_call_target="InvertDiagBlocksLowerTriangular" | custom-call | tf_op jit(solution)/shard_map/jit(cholesky)/cholesky | solution.py:111
  135.7 11.7 %cholesky.327 = f32[128,128]{1,0:T(8,128)S(1)} custom-call(f32[128,128]{1,0:T(8,128)S(1)} %convolution_subtract_fusion.6), custom_call_target="Cholesky" | custom-call | tf_op jit(solution)/shard_map/jit(cholesky)/cholesky | solution.py:111
  152.5 17.8 %while.1 = (s32[]{:T(128)}, f32[640,640]{1,0:T(8,128)}, s32[5,2]{0,1:T(2,128)S(1)}, f32[5,128,128]{2,1,0:T(8,128)}, s32[]{:T(128)}) while((s32[]{:T(128)}, f32[640,640]{1,0:T(8,128)}, s32[5,2]{0,1:T(2,128)S(1)}, f32[5,128,128]{2,1,0:T(8,128)}, s32[]{:T(128)}) %tuple.96), condition=%wide.while_cond, body=%wide.while_body.sunk | while | flops 2 | bytes 132705 | solution.py:112
  153.6 2.8 bitcast_dynamic-update-slice_fusion.2
  157.1 2.8 bitcast_dynamic-update-slice_fusion.2
  160.5 2.8 bitcast_dynamic-update-slice_fusion.2
  164.0 2.8 bitcast_dynamic-update-slice_fusion.2
  167.5 2.8 bitcast_dynamic-update-slice_fusion.2
  170.3 50.7 %custom-call.42 = f32[5,128,128]{1,2,0:T(8,128)} custom-call(f32[5,128,128]{2,1,0:T(8,128)} %get-tuple-element.10), custom_call_target="InvertDiagBlocksLowerTriangular" | custom-call | tf_op jit(solution)/shard_map/triangular_solve | solution.py:112
  234.1 4.7 collective-permute-start.11
  238.8 5.0 fusion.240
  245.8 4.4 collective-permute-start.13
  250.2 2.6 collective-permute-done.12
  256.4 3.3 collective-permute-done.14
  260.4 3.8 collective-permute-done.15
  264.9 4.4 collective-permute-start.17
  269.3 6.9 collective-permute-done.16
  285.3 26.6 %collective-permute-done.18 = f32[3,512,256]{2,1,0:T(8,128)S(1)} collective-permute-done((f32[3,512,256]{2,1,0:T(8,128)S(1)}, f32[3,512,256]{2,1,0:T(8,128)S(1)}, u32[]{:S(2)}, u32[]{:S(2)}) %collective-permute-start.18) | collective-permute-done | bytes 1572896 | tf_op jit(solution)/shard_map/ppermute | solution.py:24
  317.4 2.0 fusion.71
  321.3 2.9 multiply_reduce_fusion.4
  324.2 41.0 %all-reduce.1 = (f32[256]{0:T(256)S(1)}, f32[256]{0:T(256)S(1)}) all-reduce(f32[256]{0:T(256)S(1)} %get-tuple-element.12, f32[256]{0:T(256)S(1)} %get-tuple-element.11), channel_id=1, replica_groups=mesh['gx'=16,'gy'=2] {'gx','gy'}, use_global_device_ids=true, to_apply=%region_11.13 | all-reduce | flops 512 | bytes 4096 | tf_op jit(solution)/shard_map/psum | solution.py:64
  369.6 5.2 collective-permute-done.20
  374.7 4.8 collective-permute-done.21
  380.9 4.6 collective-permute-start.23
  391.3 4.1 collective-permute-start.25
  395.4 2.7 collective-permute-done.24
  398.2 4.4 collective-permute-start.26
  404.5 7.1 collective-permute-done.26
  412.3 3.5 collective-permute-done.27
  417.2 36.8 %psum.44 = f32[256]{0:T(256)S(1)} all-reduce(f32[256]{0:T(256)S(1)} %get-tuple-element.128), channel_id=1, replica_groups=mesh['gx'=16,'gy'=2] {'gx','gy'}, use_global_device_ids=true, to_apply=%region_15.17 | all-reduce | flops 256 | bytes 2048 | tf_op jit(solution)/shard_map/psum | solution.py:64
  455.2 4.4 collective-permute-start.29
  459.6 7.0 collective-permute-done.28
  466.7 4.3 collective-permute-start.30
  478.3 24.6 %collective-permute-done.30 = f32[3,512,256]{2,1,0:T(8,128)S(1)} collective-permute-done((f32[3,512,256]{2,1,0:T(8,128)S(1)}, f32[3,512,256]{2,1,0:T(8,128)S(1)}, u32[]{:S(2)}, u32[]{:S(2)}) %collective-permute-start.30) | collective-permute-done | bytes 1572896 | tf_op jit(solution)/shard_map/ppermute | solution.py:24
  512.3 2.8 multiply_reduce_fusion.2
  515.2 43.2 %psum.45 = f32[256]{0:T(256)S(1)} all-reduce(f32[256]{0:T(256)S(1)} %get-tuple-element.130), channel_id=1, replica_groups=mesh['gx'=16,'gy'=2] {'gx','gy'}, use_global_device_ids=true, to_apply=%region_17.19 | all-reduce | flops 256 | bytes 2048 | tf_op jit(solution)/shard_map/psum | solution.py:176
  562.8 5.2 collective-permute-done.32
  568.0 4.8 collective-permute-done.33
  574.2 4.6 collective-permute-start.35
  584.5 4.1 collective-permute-start.37
  588.7 2.7 collective-permute-done.36
  591.4 4.4 collective-permute-start.38
  597.8 6.8 collective-permute-done.38
  605.2 3.5 collective-permute-done.39
  609.4 36.9 %psum.46 = f32[256]{0:T(256)S(1)} all-reduce(f32[256]{0:T(256)S(1)} %get-tuple-element.132), channel_id=1, replica_groups=mesh['gx'=16,'gy'=2] {'gx','gy'}, use_global_device_ids=true, to_apply=%region_19.21 | all-reduce | flops 256 | bytes 2048 | tf_op jit(solution)/shard_map/psum | solution.py:64
  646.4 4.4 collective-permute-start.41
  650.8 7.0 collective-permute-done.40
  657.9 4.3 collective-permute-start.42
  669.3 25.0 %collective-permute-done.42 = f32[3,512,256]{2,1,0:T(8,128)S(1)} collective-permute-done((f32[3,512,256]{2,1,0:T(8,128)S(1)}, f32[3,512,256]{2,1,0:T(8,128)S(1)}, u32[]{:S(2)}, u32[]{:S(2)}) %collective-permute-start.42) | collective-permute-done | bytes 1572896 | tf_op jit(solution)/shard_map/ppermute | solution.py:24
  699.8 2.1 fusion.59
  703.8 2.1 multiply_reduce_fusion
  705.9 43.1 %psum.47 = f32[256]{0:T(256)S(1)} all-reduce(f32[256]{0:T(256)S(1)} %get-tuple-element.134), channel_id=1, replica_groups=mesh['gx'=16,'gy'=2] {'gx','gy'}, use_global_device_ids=true, to_apply=%region_21.23 | all-reduce | flops 256 | bytes 2048 | tf_op jit(solution)/shard_map/psum | solution.py:176
  (239 shorter events, 132.9 us)
Async XLA Ops:
  0.6 13.0 %copy-start.7 = (s32[1,1,128]{2,1,0:T(1,128)S(1)}, s32[1,1,128]{2,1,0:T(1,128)}, u32[]{:S(2)}) copy-start(s32[1,1,128]{2,1,0:T(1,128)} %param.9) | copy-start | bytes 1540
  0.6 19.3 %copy-start = (f32[1,1,512,256]{3,2,1,0:T(8,128)S(1)}, f32[1,1,512,256]{3,2,1,0:T(8,128)}, u32[]{:S(2)}) copy-start(f32[1,1,512,256]{3,2,1,0:T(8,128)} %param.6) | copy-start | bytes 1572868
  0.7 13.4 %collective-permute-start.4 = (s32[128]{0:T(128)}, s32[128]{0:T(128)S(1)}, u32[]{:S(2)}, u32[]{:S(2)}) collective-permute-start(s32[128]{0:T(128)} %bitcast.373), channel_id=1, source_target_pairs={{0,2},{2,4},{4,6},{6,8},{8,10},{10,12},{12,14},{14,16},{16,18},{18... | collective-permute-start | bytes 1544 | tf_op jit(solution)/shard_map/ppermute | solution.py:18
  1.2 12.8 %collective-permute-start.5 = (s32[128]{0:T(128)}, s32[128]{0:T(128)S(1)}, u32[]{:S(2)}, u32[]{:S(2)}) collective-permute-start(s32[128]{0:T(128)} %bitcast.374), channel_id=1, source_target_pairs={{0,30},{2,0},{4,2},{6,4},{8,6},{10,8},{12,10},{14,12},{16,14},{18,... | collective-permute-start | bytes 1544 | tf_op jit(solution)/shard_map/ppermute | solution.py:18
  7.0 16.5 %collective-permute-start = (f32[3,512]{1,0:T(4,128)S(1)}, f32[3,512]{1,0:T(4,128)S(1)}, u32[]{:S(2)}, u32[]{:S(2)}) collective-permute-start(f32[3,512]{1,0:T(4,128)S(1)} %get-tuple-element.110), channel_id=1, source_target_pairs={{0,2},{2,4},{4,6},{6,8},{8,10},{10,12},{12,14},{14,16},{16,18},{18... | collective-permute-start | bytes 18440 | tf_op jit(solution)/shard_map/ppermute | solution.py:18
  7.0 16.4 %collective-permute-start.1 = (f32[3,512]{1,0:T(4,128)S(1)}, f32[3,512]{1,0:T(4,128)S(1)}, u32[]{:S(2)}, u32[]{:S(2)}) collective-permute-start(f32[3,512]{1,0:T(4,128)S(1)} %get-tuple-element.110), channel_id=1, source_target_pairs={{0,30},{2,0},{4,2},{6,4},{8,6},{10,8},{12,10},{14,12},{16,14},{18,... | collective-permute-start | bytes 18440 | tf_op jit(solution)/shard_map/ppermute | solution.py:18
  14.1 6.7 collective-permute-start.7
  15.4 6.3 collective-permute-start.6
  23.5 208.1 %collective-permute-start.8 = (f32[3,128,256]{2,1,0:T(8,128)}, f32[3,128,256]{2,1,0:T(8,128)}, u32[]{:S(2)}, u32[]{:S(2)}) collective-permute-start(f32[3,128,256]{2,1,0:T(8,128)} %pad_maximum_fusion.3), channel_id=1, source_target_pairs={{0,30},{2,0},{4,2},{6,4},{8,6},{10,8},{12,10},{14,12},{16,14},{18,... | collective-permute-start | bytes 1179656 | tf_op jit(solution)/shard_map/ppermute | solution.py:18
  23.5 7.5 collective-permute-start.2
  27.2 5.7 collective-permute-start.3
  29.3 5.1 copy-start.6
  29.3 5.1 copy-start.8
  29.3 202.3 %collective-permute-start.9 = (f32[3,128,256]{2,1,0:T(8,128)}, f32[3,128,256]{2,1,0:T(8,128)}, u32[]{:S(2)}, u32[]{:S(2)}) collective-permute-start(f32[3,128,256]{2,1,0:T(8,128)} %pad_maximum_fusion.4), channel_id=1, source_target_pairs={{0,2},{2,4},{4,6},{6,8},{8,10},{10,12},{12,14},{14,16},{16,18},{18... | collective-permute-start | bytes 1179656 | tf_op jit(solution)/shard_map/ppermute | solution.py:18
  37.5 1.2 copy-start.4
  170.3 54.7 %copy-start.3 = (f32[640,640]{1,0:T(8,128)S(1)}, f32[640,640]{1,0:T(8,128)}, u32[]{:S(2)}) copy-start(f32[640,640]{1,0:T(8,128)} %fusion.25) | copy-start | bytes 4915204
  222.2 4.3 copy-start.5
  232.8 11.1 %collective-permute-start.10 = (f32[128,256]{1,0:T(8,128)S(1)}, f32[128,256]{1,0:T(8,128)S(1)}, u32[]{:S(2)}, u32[]{:S(2)}) collective-permute-start(f32[128,256]{1,0:T(8,128)S(1)} %get-tuple-element.60), channel_id=1, source_target_pairs={{1,0},{3,2},{5,4},{7,6},{9,8},{11,10},{13,12},{15,14},{17,16},{19,... | collective-permute-start | bytes 393224 | tf_op jit(solution)/shard_map/ppermute | solution.py:24
  234.1 9.8 %collective-permute-start.11 = (f32[128,256]{1,0:T(8,128)S(1)}, f32[128,256]{1,0:T(8,128)S(1)}, u32[]{:S(2)}, u32[]{:S(2)}) collective-permute-start(f32[128,256]{1,0:T(8,128)S(1)} %get-tuple-element.61), channel_id=1, source_target_pairs={{0,1},{2,3},{4,5},{6,7},{8,9},{10,11},{12,13},{14,15},{16,17},{18,... | collective-permute-start | bytes 393224 | tf_op jit(solution)/shard_map/ppermute | solution.py:24
  245.7 7.1 collective-permute-start.12
  245.8 7.1 collective-permute-start.13
  252.9 6.9 collective-permute-start.14
  254.5 9.7 %collective-permute-start.15 = (f32[3,128,256]{2,1,0:T(8,128)S(1)}, f32[3,128,256]{2,1,0:T(8,128)S(1)}, u32[]{:S(2)}, u32[]{:S(2)}) collective-permute-start(f32[3,128,256]{2,1,0:T(8,128)S(1)} %pad_maximum_fusion.5), channel_id=1, source_target_pairs={{1,0},{3,2},{5,4},{7,6},{9,8},{11,10},{13,12},{15,14},{17,16},{19,... | collective-permute-start | bytes 1179656 | tf_op jit(solution)/shard_map/ppermute | solution.py:24
  264.8 11.5 %collective-permute-start.16 = (f32[512,256]{1,0:T(8,128)S(1)}, f32[512,256]{1,0:T(8,128)S(1)}, u32[]{:S(2)}, u32[]{:S(2)}) collective-permute-start(f32[512,256]{1,0:T(8,128)S(1)} %convolution_add_fusion.5), channel_id=1, source_target_pairs={{0,2},{2,4},{4,6},{6,8},{8,10},{10,12},{12,14},{14,16},{16,18},{18... | collective-permute-start | bytes 1572872 | tf_op jit(solution)/shard_map/ppermute | solution.py:18
  264.9 11.4 %collective-permute-start.17 = (f32[512,256]{1,0:T(8,128)S(1)}, f32[512,256]{1,0:T(8,128)S(1)}, u32[]{:S(2)}, u32[]{:S(2)}) collective-permute-start(f32[512,256]{1,0:T(8,128)S(1)} %convolution_add_fusion.5), channel_id=1, source_target_pairs={{0,30},{2,0},{4,2},{6,4},{8,6},{10,8},{12,10},{14,12},{16,14},{18,... | collective-permute-start | bytes 1572872 | tf_op jit(solution)/shard_map/ppermute | solution.py:18
  276.4 35.5 %collective-permute-start.18 = (f32[3,512,256]{2,1,0:T(8,128)S(1)}, f32[3,512,256]{2,1,0:T(8,128)S(1)}, u32[]{:S(2)}, u32[]{:S(2)}) collective-permute-start(f32[3,512,256]{2,1,0:T(8,128)S(1)} %pad_maximum_fusion), channel_id=1, source_target_pairs={{0,1},{2,3},{4,5},{6,7},{8,9},{10,11},{12,13},{14,15},{16,17},{18,... | collective-permute-start | bytes 4718600 | tf_op jit(solution)/shard_map/ppermute | solution.py:24
  278.0 39.4 %collective-permute-start.19 = (f32[3,512,256]{2,1,0:T(8,128)S(1)}, f32[3,512,256]{2,1,0:T(8,128)S(1)}, u32[]{:S(2)}, u32[]{:S(2)}) collective-permute-start(f32[3,512,256]{2,1,0:T(8,128)S(1)} %pad_maximum_fusion), channel_id=1, source_target_pairs={{1,0},{3,2},{5,4},{7,6},{9,8},{11,10},{13,12},{15,14},{17,16},{19,... | collective-permute-start | bytes 4718600 | tf_op jit(solution)/shard_map/ppermute | solution.py:24
  368.9 5.8 collective-permute-start.20
  369.5 10.1 %collective-permute-start.21 = (f32[3,128,256]{2,1,0:T(8,128)S(1)}, f32[3,128,256]{2,1,0:T(8,128)S(1)}, u32[]{:S(2)}, u32[]{:S(2)}) collective-permute-start(f32[3,128,256]{2,1,0:T(8,128)S(1)} %pad_maximum_fusion.7), channel_id=1, source_target_pairs={{0,2},{2,4},{4,6},{6,8},{8,10},{10,12},{12,14},{14,16},{16,18},{18... | collective-permute-start | bytes 1179656 | tf_op jit(solution)/shard_map/ppermute | solution.py:18
  379.6 7.7 %collective-permute-start.22 = (f32[128,256]{1,0:T(8,128)S(1)}, f32[128,256]{1,0:T(8,128)S(1)}, u32[]{:S(2)}, u32[]{:S(2)}) collective-permute-start(f32[128,256]{1,0:T(8,128)S(1)} %get-tuple-element.49), channel_id=1, source_target_pairs={{1,0},{3,2},{5,4},{7,6},{9,8},{11,10},{13,12},{15,14},{17,16},{19,... | collective-permute-start | bytes 393224 | tf_op jit(solution)/shard_map/ppermute | solution.py:24
  380.9 8.2 %collective-permute-start.23 = (f32[128,256]{1,0:T(8,128)S(1)}, f32[128,256]{1,0:T(8,128)S(1)}, u32[]{:S(2)}, u32[]{:S(2)}) collective-permute-start(f32[128,256]{1,0:T(8,128)S(1)} %get-tuple-element.50), channel_id=1, source_target_pairs={{0,1},{2,3},{4,5},{6,7},{8,9},{10,11},{12,13},{14,15},{16,17},{18,... | collective-permute-start | bytes 393224 | tf_op jit(solution)/shard_map/ppermute | solution.py:24
  390.9 7.2 collective-permute-start.24
  391.3 6.8 collective-permute-start.25
  398.2 13.5 %collective-permute-start.26 = (f32[3,128,256]{2,1,0:T(8,128)S(1)}, f32[3,128,256]{2,1,0:T(8,128)S(1)}, u32[]{:S(2)}, u32[]{:S(2)}) collective-permute-start(f32[3,128,256]{2,1,0:T(8,128)S(1)} %pad_maximum_fusion.8), channel_id=1, source_target_pairs={{0,1},{2,3},{4,5},{6,7},{8,9},{10,11},{12,13},{14,15},{16,17},{18,... | collective-permute-start | bytes 1179656 | tf_op jit(solution)/shard_map/ppermute | solution.py:24
  402.6 13.2 %collective-permute-start.27 = (f32[3,128,256]{2,1,0:T(8,128)S(1)}, f32[3,128,256]{2,1,0:T(8,128)S(1)}, u32[]{:S(2)}, u32[]{:S(2)}) collective-permute-start(f32[3,128,256]{2,1,0:T(8,128)S(1)} %pad_maximum_fusion.8), channel_id=1, source_target_pairs={{1,0},{3,2},{5,4},{7,6},{9,8},{11,10},{13,12},{15,14},{17,16},{19,... | collective-permute-start | bytes 1179656 | tf_op jit(solution)/shard_map/ppermute | solution.py:24
  455.1 57.2 %copy-start.1 = (f32[512,256]{1,0:T(8,128)}, f32[512,256]{1,0:T(8,128)S(1)}, u32[]{:S(2)}) copy-start(f32[512,256]{1,0:T(8,128)S(1)} %multiply_add_fusion.1) | copy-start | bytes 1572868
  455.1 11.5 %collective-permute-start.28 = (f32[512,256]{1,0:T(8,128)S(1)}, f32[512,256]{1,0:T(8,128)S(1)}, u32[]{:S(2)}, u32[]{:S(2)}) collective-permute-start(f32[512,256]{1,0:T(8,128)S(1)} %multiply_add_fusion.1), channel_id=1, source_target_pairs={{0,2},{2,4},{4,6},{6,8},{8,10},{10,12},{12,14},{14,16},{16,18},{18... | collective-permute-start | bytes 1572872 | tf_op jit(solution)/shard_map/ppermute | solution.py:18
  455.2 11.4 %collective-permute-start.29 = (f32[512,256]{1,0:T(8,128)S(1)}, f32[512,256]{1,0:T(8,128)S(1)}, u32[]{:S(2)}, u32[]{:S(2)}) collective-permute-start(f32[512,256]{1,0:T(8,128)S(1)} %multiply_add_fusion.1), channel_id=1, source_target_pairs={{0,30},{2,0},{4,2},{6,4},{8,6},{10,8},{12,10},{14,12},{16,14},{18,... | collective-permute-start | bytes 1572872 | tf_op jit(solution)/shard_map/ppermute | solution.py:18
  466.7 36.1 %collective-permute-start.30 = (f32[3,512,256]{2,1,0:T(8,128)S(1)}, f32[3,512,256]{2,1,0:T(8,128)S(1)}, u32[]{:S(2)}, u32[]{:S(2)}) collective-permute-start(f32[3,512,256]{2,1,0:T(8,128)S(1)} %pad_maximum_fusion.1), channel_id=1, source_target_pairs={{0,1},{2,3},{4,5},{6,7},{8,9},{10,11},{12,13},{14,15},{16,17},{18,... | collective-permute-start | bytes 4718600 | tf_op jit(solution)/shard_map/ppermute | solution.py:24
  471.0 37.4 %collective-permute-start.31 = (f32[3,512,256]{2,1,0:T(8,128)S(1)}, f32[3,512,256]{2,1,0:T(8,128)S(1)}, u32[]{:S(2)}, u32[]{:S(2)}) collective-permute-start(f32[3,512,256]{2,1,0:T(8,128)S(1)} %pad_maximum_fusion.1), channel_id=1, source_target_pairs={{1,0},{3,2},{5,4},{7,6},{9,8},{11,10},{13,12},{15,14},{17,16},{19,... | collective-permute-start | bytes 4718600 | tf_op jit(solution)/shard_map/ppermute | solution.py:24
  562.1 5.9 collective-permute-start.32
  562.7 10.1 %collective-permute-start.33 = (f32[3,128,256]{2,1,0:T(8,128)S(1)}, f32[3,128,256]{2,1,0:T(8,128)S(1)}, u32[]{:S(2)}, u32[]{:S(2)}) collective-permute-start(f32[3,128,256]{2,1,0:T(8,128)S(1)} %pad_maximum_fusion.10), channel_id=1, source_target_pairs={{0,2},{2,4},{4,6},{6,8},{8,10},{10,12},{12,14},{14,16},{16,18},{18... | collective-permute-start | bytes 1179656 | tf_op jit(solution)/shard_map/ppermute | solution.py:18
  572.9 7.8 %collective-permute-start.34 = (f32[128,256]{1,0:T(8,128)S(1)}, f32[128,256]{1,0:T(8,128)S(1)}, u32[]{:S(2)}, u32[]{:S(2)}) collective-permute-start(f32[128,256]{1,0:T(8,128)S(1)} %get-tuple-element.38), channel_id=1, source_target_pairs={{1,0},{3,2},{5,4},{7,6},{9,8},{11,10},{13,12},{15,14},{17,16},{19,... | collective-permute-start | bytes 393224 | tf_op jit(solution)/shard_map/ppermute | solution.py:24
  574.2 8.2 %collective-permute-start.35 = (f32[128,256]{1,0:T(8,128)S(1)}, f32[128,256]{1,0:T(8,128)S(1)}, u32[]{:S(2)}, u32[]{:S(2)}) collective-permute-start(f32[128,256]{1,0:T(8,128)S(1)} %get-tuple-element.39), channel_id=1, source_target_pairs={{0,1},{2,3},{4,5},{6,7},{8,9},{10,11},{12,13},{14,15},{16,17},{18,... | collective-permute-start | bytes 393224 | tf_op jit(solution)/shard_map/ppermute | solution.py:24
  584.2 7.2 collective-permute-start.36
  584.5 6.9 collective-permute-start.37
  591.4 13.1 %collective-permute-start.38 = (f32[3,128,256]{2,1,0:T(8,128)S(1)}, f32[3,128,256]{2,1,0:T(8,128)S(1)}, u32[]{:S(2)}, u32[]{:S(2)}) collective-permute-start(f32[3,128,256]{2,1,0:T(8,128)S(1)} %pad_maximum_fusion.11), channel_id=1, source_target_pairs={{0,1},{2,3},{4,5},{6,7},{8,9},{10,11},{12,13},{14,15},{16,17},{18,... | collective-permute-start | bytes 1179656 | tf_op jit(solution)/shard_map/ppermute | solution.py:24
  595.9 12.8 %collective-permute-start.39 = (f32[3,128,256]{2,1,0:T(8,128)S(1)}, f32[3,128,256]{2,1,0:T(8,128)S(1)}, u32[]{:S(2)}, u32[]{:S(2)}) collective-permute-start(f32[3,128,256]{2,1,0:T(8,128)S(1)} %pad_maximum_fusion.11), channel_id=1, source_target_pairs={{1,0},{3,2},{5,4},{7,6},{9,8},{11,10},{13,12},{15,14},{17,16},{19,... | collective-permute-start | bytes 1179656 | tf_op jit(solution)/shard_map/ppermute | solution.py:24
  605.2 41.1 %copy-start.2 = (f32[512,256]{1,0:T(8,128)S(1)}, f32[512,256]{1,0:T(8,128)}, u32[]{:S(2)}) copy-start(f32[512,256]{1,0:T(8,128)} %copy-done.1) | copy-start | bytes 1572868
  646.3 11.5 %collective-permute-start.40 = (f32[512,256]{1,0:T(8,128)S(1)}, f32[512,256]{1,0:T(8,128)S(1)}, u32[]{:S(2)}, u32[]{:S(2)}) collective-permute-start(f32[512,256]{1,0:T(8,128)S(1)} %multiply_add_fusion), channel_id=1, source_target_pairs={{0,2},{2,4},{4,6},{6,8},{8,10},{10,12},{12,14},{14,16},{16,18},{18... | collective-permute-start | bytes 1572872 | tf_op jit(solution)/shard_map/ppermute | solution.py:18
  646.4 11.4 %collective-permute-start.41 = (f32[512,256]{1,0:T(8,128)S(1)}, f32[512,256]{1,0:T(8,128)S(1)}, u32[]{:S(2)}, u32[]{:S(2)}) collective-permute-start(f32[512,256]{1,0:T(8,128)S(1)} %multiply_add_fusion), channel_id=1, source_target_pairs={{0,30},{2,0},{4,2},{6,4},{8,6},{10,8},{12,10},{14,12},{16,14},{18,... | collective-permute-start | bytes 1572872 | tf_op jit(solution)/shard_map/ppermute | solution.py:18
  657.9 36.3 %collective-permute-start.42 = (f32[3,512,256]{2,1,0:T(8,128)S(1)}, f32[3,512,256]{2,1,0:T(8,128)S(1)}, u32[]{:S(2)}, u32[]{:S(2)}) collective-permute-start(f32[3,512,256]{2,1,0:T(8,128)S(1)} %pad_maximum_fusion.2), channel_id=1, source_target_pairs={{0,1},{2,3},{4,5},{6,7},{8,9},{10,11},{12,13},{14,15},{16,17},{18,... | collective-permute-start | bytes 4718600 | tf_op jit(solution)/shard_map/ppermute | solution.py:24
  662.2 37.6 %collective-permute-start.43 = (f32[3,512,256]{2,1,0:T(8,128)S(1)}, f32[3,512,256]{2,1,0:T(8,128)S(1)}, u32[]{:S(2)}, u32[]{:S(2)}) collective-permute-start(f32[3,512,256]{2,1,0:T(8,128)S(1)} %pad_maximum_fusion.2), channel_id=1, source_target_pairs={{1,0},{3,2},{5,4},{7,6},{9,8},{11,10},{13,12},{15,14},{17,16},{19,... | collective-permute-start | bytes 4718600 | tf_op jit(solution)/shard_map/ppermute | solution.py:24
where the time goes:
time: 756 us; the launch traced here: 751 us
  blocking collectives  201 us (27%)
  other arithmetic  168 us (22%)
  waiting for transfers between devices  161 us (21%)
  starting transfers between devices  96.9 us (13%)
  matrix products  94.9 us (13%)
  local copies, waits for them, and re-layouts  22.5 us (3%)
    psum x3, blocking collectives, residual_dot(): return lax.psum(column_sum(residue, precond), ('gx', 'gy'))  115 us
    ppermute x22, waiting for transfers between devices, passed_along(): return lax.ppermute(block, axis, route)  112 us
    another operation x19, other arithmetic, shards(): factor = jnp.linalg.cholesky(local_matrix)  101 us
    psum x2, blocking collectives, shards(): lax.psum(column_sum(direction, accumulated), ('gx', 'gy'))  86.3 us
    ppermute x22, starting transfers between devices, passed_along(): return lax.ppermute(block, axis, route)  57.9 us
    dot_general x27, matrix products, shards(): jnp.dot(kernel_block(own_pos, positions[operate_row_off][operate_col_off]...  52.9 us
    another operation x3, other arithmetic, shards(): lax.linalg.triangular_solve(factor, jnp.eye(ext_len, dtype=jnp.float32),...  52 us
    ppermute x22, waiting for transfers between devices, shifted(): lax.ppermute(value, axis, [(i, (i + by) % count) for i in range(count)])  49 us
  transfers between devices with their start and end apart: 44, of which 24 were waited for; matrix products, arithmetic and copies ran while one was open for 33% of the time, Pallas kernels for 0%

commit v1 on v0

--- a/solution.py
+++ b/solution.py
@@ -1,8 +1,11 @@
+import functools
 import math
 
 import jax
 import jax.numpy as jnp
 from jax import lax
+from jax.experimental import pallas as pl
+from jax.experimental.pallas import tpu as pltpu
 from jax.sharding import PartitionSpec as P
 
 ITERS = 3
@@ -56,12 +59,131 @@
     return [across[1], column, across[-1]]
 
 
-def column_sum(first, second):
-    return jnp.sum(first * second, axis=0)
-
-
-def residual_dot(residue, precond):
-    return lax.psum(column_sum(residue, precond), ("gx", "gy"))
+MESH = pl.DeviceIdType.MESH
+NOISE_MIN = 0.25
+VMEM = pl.BlockSpec(memory_space=pltpu.VMEM)
+
+
+def split(value):
+    top = value.astype(jnp.bfloat16)
+    return top, (value - top.astype(jnp.float32)).astype(jnp.bfloat16)
+
+
+def dot3(left, right):
+    left_top, left_low = split(left)
+    right_top, right_low = split(right)
+    return jnp.dot(
+        jnp.concatenate([left_top, left_top, left_low], axis=1),
+        jnp.concatenate([right_top, right_low, right_top], axis=0),
+        preferred_element_type=jnp.float32,
+    )
+
+
+def dot6(left, right):
+    return jnp.dot(left, right, precision=HIGH, preferred_element_type=jnp.float32)
+
+
+def block_inverse(block):
+    size = block.shape[0]
+    low, high = NOISE_MIN * 0.97, (size + 1.0) * 1.01
+    eye = (
+        lax.broadcasted_iota(jnp.int32, block.shape, 0)
+        == lax.broadcasted_iota(jnp.int32, block.shape, 1)
+    ).astype(jnp.float32)
+    first = 2.0 / (low + high)
+    gap = 1.0 - first * low
+    scale = 2.0 / (2.0 - gap * gap)
+    guess = (2.0 * first * scale) * eye - (first * first * scale) * block
+    gap = gap * gap / (2.0 - gap * gap)
+    while gap > 1e-3:
+        scale = 2.0 / (2.0 - gap * gap)
+        rest = 2.0 * eye - dot3(block, guess)
+        guess = scale * dot3(guess, rest)
+        gap = gap * gap / (2.0 - gap * gap)
+    for _ in range(2):
+        guess = guess + dot3(guess, eye - dot6(block, guess))
+    return guess
+
+
+def inverse_kernel(step, matrix_ref, out_ref):
+    size = matrix_ref.shape[0]
+    out_ref[...] = matrix_ref[...]
+    for start in range(0, size, step):
+        here = slice(start, start + step)
+        pivot = block_inverse(out_ref[here, here])
+        column = out_ref[:, here]
+        row = dot6(pivot, out_ref[here, :])
+        for low in range(0, size, step):
+            if low != start:
+                part = slice(low, low + step)
+                out_ref[part, :] = out_ref[part, :] - dot6(column[part], row)
+                out_ref[part, here] = -dot6(column[part], pivot)
+        out_ref[here, :] = row
+        out_ref[here, here] = pivot
+
+
+def spd_inverse(matrix):
+    size = matrix.shape[0]
+    step = math.gcd(size, 128)
+    return pl.pallas_call(
+        functools.partial(inverse_kernel, step),
+        out_shape=jax.ShapeDtypeStruct(matrix.shape, jnp.float32),
+        in_specs=[VMEM],
+        out_specs=VMEM,
+        compiler_params=pltpu.CompilerParams(vmem_limit_bytes=32 * 1024 * 1024),
+    )(matrix)
+
+
+def sum_kernel(axes, left_ref, right_ref, out_ref, mine, *rest):
+    slots, (send_sem, recv_sem) = rest[: len(axes)], rest[len(axes) :]
+    barrier = pltpu.get_barrier_semaphore()
+    greeted = 0
+    for axis in axes:
+        count = lax.axis_size(axis)
+        for hop in range(1, count):
+            other = lax.rem(lax.axis_index(axis) + hop, count)
+            pl.semaphore_signal(barrier, inc=1, device_id={axis: other}, device_id_type=MESH)
+            greeted += 1
+    mine[0] = jnp.sum(left_ref[...] * right_ref[...], axis=0, keepdims=True)
+    pl.semaphore_wait(barrier, greeted)
+    for stage, axis in enumerate(axes):
+        count = lax.axis_size(axis)
+        copies = []
+        for hop in range(1, count):
+            other = lax.rem(lax.axis_index(axis) + hop, count)
+            copy = pltpu.make_async_remote_copy(
+                src_ref=mine.at[stage],
+                dst_ref=slots[stage].at[hop - 1],
+                send_sem=send_sem.at[stage],
+                recv_sem=recv_sem.at[stage],
+                device_id={axis: other},
+                device_id_type=MESH,
+            )
+            copy.start()
+            copies.append(copy)
+        if copies:
+            whole = pltpu.make_async_copy(slots[stage], slots[stage], recv_sem.at[stage])
+            whole.wait()
+            mine[stage + 1] = mine[stage] + jnp.sum(slots[stage][...], axis=0)
+            pltpu.make_async_copy(slots[stage], slots[stage], send_sem.at[stage]).wait()
+        else:
+            mine[stage + 1] = mine[stage]
+    out_ref[...] = mine[len(axes)]
+
+
+def total_dot(first, second):
+    axes = ("gy", "gx")
+    width = first.shape[1]
+    return pl.pallas_call(
+        functools.partial(sum_kernel, axes),
+        out_shape=jax.ShapeDtypeStruct((1, width), jnp.float32),
+        in_specs=[VMEM, VMEM],
+        out_specs=VMEM,
+        scratch_shapes=[pltpu.VMEM((len(axes) + 1, 1, width), jnp.float32)]
+        + [pltpu.VMEM((max(lax.axis_size(a) - 1, 1), 1, width), jnp.float32) for a in axes]
+        + [pltpu.SemaphoreType.DMA((len(axes),)), pltpu.SemaphoreType.DMA((len(axes),))],
+        compiler_params=pltpu.CompilerParams(collective_id=0, has_side_effects=True),
+    )(first, second)[0]
 
 
 def shards(right_side, coords, noise, intersect):
@@ -108,11 +230,7 @@
     ext_pos = jnp.concatenate([own_pos, ov_pos], axis=1)
     ext_noise = jnp.concatenate([own_noise, chosen[2]])
     local_matrix = kernel_block(ext_pos, ext_pos) + jnp.diag(ext_noise)
-    factor = jnp.linalg.cholesky(local_matrix)
-    inv_factor = lax.linalg.triangular_solve(
-        factor, jnp.eye(ext_len, dtype=jnp.float32), left_side=True, lower=True
-    )
-    inverse = jnp.dot(inv_factor.T, inv_factor, precision=HIGH, preferred_element_type=jnp.float32)
+    inverse = spd_inverse(local_matrix)
     near_ids = window_index(intersect_ids)
     point_iota = jnp.arange(points, dtype=jnp.int32)[:, None]
     row_base = (2 - jnp.arange(3, dtype=jnp.int32))[:, None] * 3
@@ -161,7 +279,7 @@
     solution = jnp.zeros_like(residual)
     precond = precondition(residual)
     direction = precond
-    inner_now = residual_dot(residual, precond)
+    inner_now = total_dot(residual, precond)
     for iteration in range(ITERS):
         columns = window_values(direction)
         accumulated = noise_col * direction
@@ -173,12 +291,12 @@
                     precision=HIGH,
                     preferred_element_type=jnp.float32,
                 )
-        step_size = inner_now / lax.psum(column_sum(direction, accumulated), ("gx", "gy"))
+        step_size = inner_now / total_dot(direction, accumulated)
         solution = solution + step_size * direction
         residual = residual - step_size * accumulated
         if iteration + 1 < ITERS:
             precond = precondition(residual)
-            inner_next = residual_dot(residual, precond)
+            inner_next = total_dot(residual, precond)
             direction = precond + inner_next / inner_now * direction
             inner_now = inner_next
     return (solution.reshape(1, 1, points, rhs_count), residual.reshape(1, 1, points, rhs_count))

time: 756 us -> 467 us (0.62)
  blocking collectives: 201 us -> 0 us
  other arithmetic: 168 us -> 18 us
  Pallas kernels: 0 us -> 122 us
  waiting for transfers between devices: 161 us -> 133 us
  local copies, waits for them, and re-layouts: 22.5 us -> 4.55 us
  matrix products: 94.9 us -> 81.5 us
    psum x5 -> x0, blocking collectives: 201 us -> none  [the longest x3 115 us: residual_dot(): return lax.psum(column_sum(residue, precond), ('gx', 'gy'))]
    another operation x22 -> x0, other arithmetic: 153 us -> none  [the longest x19 101 us: shards(): factor = jnp.linalg.cholesky(local_matrix)]
    pallas_call x0 -> x7, Pallas kernels: none -> 122 us  [the longest x6 99.6 us: total_dot(): pl.pallas_call(functools.partial(sum_kernel, axes), out_shape=jax.ShapeDt...]
    ppermute x22, waiting for transfers between devices: 112 us -> 79.7 us  [passed_along(): return lax.ppermute(block, axis, route)]
    another operation x17 -> x0, matrix products: 18.2 us -> none  [the longest x9 10.5 us: shards(): lax.linalg.triangular_solve(factor, jnp.eye(ext_len, dtype=jnp.float32),...]
    another operation x21 -> x0, local copies, waits for them, and re-layouts: 17.5 us -> none
    dot_general x27, matrix products: 52.9 us -> 60.8 us  [shards(): jnp.dot(kernel_block(own_pos, positions[operate_row_off][operate_col_off]...]
  transfers between devices with their start and end apart: 44 -> 44, of which waited for: 24 -> 24; matrix products, arithmetic and copies ran while one was open for 33% -> 12% of each run, Pallas kernels for 0% -> 14%
where the time goes in v1:
time: 467 us; the launch traced here: 462 us
  waiting for transfers between devices  133 us (28%)
  Pallas kernels  122 us (26%)
  starting transfers between devices  101 us (22%)
  matrix products  81.5 us (17%)
  other arithmetic  18 us (4%)
    pallas_call x6, Pallas kernels, total_dot(): pl.pallas_call(functools.partial(sum_kernel, axes), out_shape=jax.ShapeDt...  99.6 us
    ppermute x22, waiting for transfers between devices, passed_along(): return lax.ppermute(block, axis, route)  79.7 us
    dot_general x27, matrix products, shards(): jnp.dot(kernel_block(own_pos, positions[operate_row_off][operate_col_off]...  60.8 us
    ppermute x22, starting transfers between devices, passed_along(): return lax.ppermute(block, axis, route)  57.2 us
    ppermute x22, waiting for transfers between devices, shifted(): lax.ppermute(value, axis, [(i, (i + by) % count) for i in range(count)])  52.8 us
    ppermute x22, starting transfers between devices, shifted(): lax.ppermute(value, axis, [(i, (i + by) % count) for i in range(count)])  43.6 us
    pallas_call x1, Pallas kernels, spd_inverse(): pl.pallas_call(functools.partial(inverse_kernel, step), out_shape=jax.Sha...  22.4 us
  transfers between devices with their start and end apart: 44, of which 24 were waited for; matrix products, arithmetic and copies ran while one was open for 12% of the time, Pallas kernels for 14%

profile of v1, /device:TPU:0, one launch (start us, length us, event | category | flops | bytes accessed | tf_op | source)
XLA Modules:
  0.0 461.7 jit_solution(16079921903739013663)
XLA Ops:
  1.2 5.0 %collective-permute-start.5 = (s32[128]{0:T(128)}, s32[128]{0:T(128)S(1)}, u32[]{:S(2)}, u32[]{:S(2)}) collective-permute-start(s32[128]{0:T(128)} %bitcast.314), channel_id=1, source_target_pairs={{0,30},{2,0},{4,2},{6,4},{8,6},{10,8},{12,10},{14,12},{16,14},{18,... | collective-permute-start | bytes 1544 | tf_op jit(solution)/shard_map/ppermute | solution.py:21
  7.0 4.4 collective-permute-start.1
  15.9 4.5 collective-permute-start.6
  24.4 2.7 collective-permute-start.2
  30.6 2.2 collective-permute-done.3
  34.3 4.2 collective-permute-done.9
  40.9 4.8 %collective-permute-start.11 = (f32[128,256]{1,0:T(8,128)S(1)}, f32[128,256]{1,0:T(8,128)S(1)}, u32[]{:S(2)}, u32[]{:S(2)}) collective-permute-start(f32[128,256]{1,0:T(8,128)S(1)} %get-tuple-element.39), channel_id=1, source_target_pairs={{0,1},{2,3},{4,5},{6,7},{8,9},{10,11},{12,13},{14,15},{16,17},{18,... | collective-permute-start | bytes 393224 | tf_op jit(solution)/shard_map/ppermute | solution.py:27
  47.1 22.4 %shard_map.59 = f32[640,640]{1,0:T(8,128)S(1)} custom-call(f32[640,640]{1,0:T(8,128)S(1)} %select_add_fusion.matrix_ref), custom_call_target="tpu_custom_call" | custom-call | tf_op jit(solution)/shard_map/pallas_call | solution.py:128
  71.4 4.4 collective-permute-start.13
  75.8 2.6 collective-permute-done.12
  81.8 3.3 collective-permute-done.14
  85.7 3.8 collective-permute-done.15
  90.2 4.4 collective-permute-start.17
  94.7 6.9 %collective-permute-done.16 = f32[512,256]{1,0:T(8,128)S(1)} collective-permute-done((f32[512,256]{1,0:T(8,128)S(1)}, f32[512,256]{1,0:T(8,128)S(1)}, u32[]{:S(2)}, u32[]{:S(2)}) %collective-permute-start.16) | collective-permute-done | bytes 524320 | tf_op jit(solution)/shard_map/ppermute | solution.py:21
  102.9 2.6 collective-permute-start.18
  106.9 42.4 %shard_map.60 = f32[1,256]{1,0:T(1,128)} custom-call(f32[512,256]{1,0:T(8,128)} %bitcast.272, f32[512,256]{1,0:T(8,128)} %copy-done.6), custom_call_target="tpu_custom_call" | custom-call | tf_op jit(solution)/shard_map/pallas_call | solution.py:177
  149.3 2.9 fusion.59
  152.2 1.9 fusion.56
  156.0 2.9 fusion.49
  158.9 2.9 fusion.50
  161.8 2.9 fusion.52
  164.7 3.1 fusion.51
  167.8 2.9 fusion.48
  170.7 3.9 fusion.8.right_ref
  174.7 9.7 %shard_map.61 = f32[1,256]{1,0:T(1,128)} custom-call(f32[512,256]{1,0:T(8,128)} %copy-done.6, f32[512,256]{1,0:T(8,128)} %fusion.8.right_ref), custom_call_target="tpu_custom_call" | custom-call | tf_op jit(solution)/shard_map/pallas_call | solution.py:177
  188.7 2.3 collective-permute-start.20
  191.2 5.2 %collective-permute-done.20 = f32[3,128,256]{2,1,0:T(8,128)S(1)} collective-permute-done((f32[3,128,256]{2,1,0:T(8,128)S(1)}, f32[3,128,256]{2,1,0:T(8,128)S(1)}, u32[]{:S(2)}, u32[]{:S(2)}) %collective-permute-start.20) | collective-permute-done | bytes 393248 | tf_op jit(solution)/shard_map/ppermute | solution.py:21
  196.4 4.7 %collective-permute-done.21 = f32[3,128,256]{2,1,0:T(8,128)S(1)} collective-permute-done((f32[3,128,256]{2,1,0:T(8,128)S(1)}, f32[3,128,256]{2,1,0:T(8,128)S(1)}, u32[]{:S(2)}, u32[]{:S(2)}) %collective-permute-start.21) | collective-permute-done | bytes 393248 | tf_op jit(solution)/shard_map/ppermute | solution.py:21
  202.5 4.6 collective-permute-start.23
  211.4 4.4 collective-permute-start.25
  215.8 2.6 collective-permute-done.24
  218.5 4.4 collective-permute-start.26
  224.8 4.9 %collective-permute-done.26 = f32[3,128,256]{2,1,0:T(8,128)S(1)} collective-permute-done((f32[3,128,256]{2,1,0:T(8,128)S(1)}, f32[3,128,256]{2,1,0:T(8,128)S(1)}, u32[]{:S(2)}, u32[]{:S(2)}) %collective-permute-start.26) | collective-permute-done | bytes 393248 | tf_op jit(solution)/shard_map/ppermute | solution.py:27
  230.3 3.5 collective-permute-done.27
  235.3 9.4 %shard_map.62 = f32[1,256]{1,0:T(1,128)} custom-call(f32[512,256]{1,0:T(8,128)} %copy-done, f32[512,256]{1,0:T(8,128)} %convolution_add_fusion.4.right_ref), custom_call_target="tpu_custom_call" | custom-call | tf_op jit(solution)/shard_map/pallas_call | solution.py:177
  246.7 4.3 collective-permute-start.29
  251.0 7.0 %collective-permute-done.28 = f32[512,256]{1,0:T(8,128)S(1)} collective-permute-done((f32[512,256]{1,0:T(8,128)S(1)}, f32[512,256]{1,0:T(8,128)S(1)}, u32[]{:S(2)}, u32[]{:S(2)}) %collective-permute-start.28) | collective-permute-done | bytes 524320 | tf_op jit(solution)/shard_map/ppermute | solution.py:21
  258.1 4.3 collective-permute-start.30
  265.9 1.9 fusion.55
  269.7 24.8 %collective-permute-done.30 = f32[3,512,256]{2,1,0:T(8,128)S(1)} collective-permute-done((f32[3,512,256]{2,1,0:T(8,128)S(1)}, f32[3,512,256]{2,1,0:T(8,128)S(1)}, u32[]{:S(2)}, u32[]{:S(2)}) %collective-permute-start.30) | collective-permute-done | bytes 1572896 | tf_op jit(solution)/shard_map/ppermute | solution.py:27
  300.1 2.0 fusion.45
  302.1 1.9 fusion.42
  304.0 2.8 fusion.6.right_ref
  306.8 14.1 %shard_map.63 = f32[1,256]{1,0:T(1,128)} custom-call(f32[512,256]{1,0:T(8,128)} %copy-done.9, f32[512,256]{1,0:T(8,128)} %fusion.6.right_ref), custom_call_target="tpu_custom_call" | custom-call | tf_op jit(solution)/shard_map/pallas_call | solution.py:177
  325.3 3.8 collective-permute-start.32
  329.3 5.2 %collective-permute-done.32 = f32[3,128,256]{2,1,0:T(8,128)S(1)} collective-permute-done((f32[3,128,256]{2,1,0:T(8,128)S(1)}, f32[3,128,256]{2,1,0:T(8,128)S(1)}, u32[]{:S(2)}, u32[]{:S(2)}) %collective-permute-start.32) | collective-permute-done | bytes 393248 | tf_op jit(solution)/shard_map/ppermute | solution.py:21
  334.5 4.7 %collective-permute-done.33 = f32[3,128,256]{2,1,0:T(8,128)S(1)} collective-permute-done((f32[3,128,256]{2,1,0:T(8,128)S(1)}, f32[3,128,256]{2,1,0:T(8,128)S(1)}, u32[]{:S(2)}, u32[]{:S(2)}) %collective-permute-start.33) | collective-permute-done | bytes 393248 | tf_op jit(solution)/shard_map/ppermute | solution.py:21
  340.6 4.6 collective-permute-start.35
  349.5 4.4 collective-permute-start.37
  353.9 2.6 collective-permute-done.36
  356.6 4.4 collective-permute-start.38
  362.9 3.5 collective-permute-done.38
  367.0 3.7 collective-permute-done.39
  372.1 9.4 %shard_map.64 = f32[1,256]{1,0:T(1,128)} custom-call(f32[512,256]{1,0:T(8,128)} %copy-done.2, f32[512,256]{1,0:T(8,128)} %convolution_add_fusion.3.right_ref), custom_call_target="tpu_custom_call" | custom-call | tf_op jit(solution)/shard_map/pallas_call | solution.py:177
  383.5 4.3 collective-permute-start.41
  387.8 7.0 %collective-permute-done.40 = f32[512,256]{1,0:T(8,128)S(1)} collective-permute-done((f32[512,256]{1,0:T(8,128)S(1)}, f32[512,256]{1,0:T(8,128)S(1)}, u32[]{:S(2)}, u32[]{:S(2)}) %collective-permute-start.40) | collective-permute-done | bytes 524320 | tf_op jit(solution)/shard_map/ppermute | solution.py:21
  394.9 4.3 collective-permute-start.42
  402.5 1.9 fusion.54
  406.3 25.0 %collective-permute-done.42 = f32[3,512,256]{2,1,0:T(8,128)S(1)} collective-permute-done((f32[3,512,256]{2,1,0:T(8,128)S(1)}, f32[3,512,256]{2,1,0:T(8,128)S(1)}, u32[]{:S(2)}, u32[]{:S(2)}) %collective-permute-start.42) | collective-permute-done | bytes 1572896 | tf_op jit(solution)/shard_map/ppermute | solution.py:27
  436.8 2.1 fusion.39
  438.9 1.9 fusion.36
  440.8 2.8 fusion.4.right_ref
  443.7 14.5 %shard_map.65 = f32[1,256]{1,0:T(1,128)} custom-call(f32[512,256]{1,0:T(8,128)} %copy-done.11, f32[512,256]{1,0:T(8,128)} %fusion.4.right_ref), custom_call_target="tpu_custom_call" | custom-call | tf_op jit(solution)/shard_map/pallas_call | solution.py:177
  458.9 2.4 subtract_bitcast_fusion
  (192 shorter events, 84.0 us)
Async XLA Ops:
  0.6 21.8 %copy-start.4 = (f32[1,1,512,256]{3,2,1,0:T(8,128)S(1)}, f32[1,1,512,256]{3,2,1,0:T(8,128)}, u32[]{:S(2)}) copy-start(f32[1,1,512,256]{3,2,1,0:T(8,128)} %param.6) | copy-start | bytes 1572868
  0.6 13.2 %collective-permute-start.4 = (s32[128]{0:T(128)}, s32[128]{0:T(128)S(1)}, u32[]{:S(2)}, u32[]{:S(2)}) collective-permute-start(s32[128]{0:T(128)} %bitcast.313), channel_id=1, source_target_pairs={{0,2},{2,4},{4,6},{6,8},{8,10},{10,12},{12,14},{14,16},{16,18},{18... | collective-permute-start | bytes 1544 | tf_op jit(solution)/shard_map/ppermute | solution.py:21
  1.2 12.7 %collective-permute-start.5 = (s32[128]{0:T(128)}, s32[128]{0:T(128)S(1)}, u32[]{:S(2)}, u32[]{:S(2)}) collective-permute-start(s32[128]{0:T(128)} %bitcast.314), channel_id=1, source_target_pairs={{0,30},{2,0},{4,2},{6,4},{8,6},{10,8},{12,10},{14,12},{16,14},{18,... | collective-permute-start | bytes 1544 | tf_op jit(solution)/shard_map/ppermute | solution.py:21
  6.9 17.4 %collective-permute-start = (f32[3,512]{1,0:T(4,128)S(1)}, f32[3,512]{1,0:T(4,128)S(1)}, u32[]{:S(2)}, u32[]{:S(2)}) collective-permute-start(f32[3,512]{1,0:T(4,128)S(1)} %get-tuple-element.75), channel_id=1, source_target_pairs={{0,2},{2,4},{4,6},{6,8},{8,10},{10,12},{12,14},{14,16},{16,18},{18... | collective-permute-start | bytes 18440 | tf_op jit(solution)/shard_map/ppermute | solution.py:21
  7.0 17.3 %collective-permute-start.1 = (f32[3,512]{1,0:T(4,128)S(1)}, f32[3,512]{1,0:T(4,128)S(1)}, u32[]{:S(2)}, u32[]{:S(2)}) collective-permute-start(f32[3,512]{1,0:T(4,128)S(1)} %get-tuple-element.75), channel_id=1, source_target_pairs={{0,30},{2,0},{4,2},{6,4},{8,6},{10,8},{12,10},{14,12},{16,14},{18,... | collective-permute-start | bytes 18440 | tf_op jit(solution)/shard_map/ppermute | solution.py:21
  14.6 7.7 %collective-permute-start.7 = (s32[3,128]{1,0:T(4,128)S(1)}, s32[3,128]{1,0:T(4,128)S(1)}, u32[]{:S(2)}, u32[]{:S(2)}) collective-permute-start(s32[3,128]{1,0:T(4,128)S(1)} %get-tuple-element.79), channel_id=1, source_target_pairs={{1,0},{3,2},{5,4},{7,6},{9,8},{11,10},{13,12},{15,14},{17,16},{19,... | collective-permute-start | bytes 4616 | tf_op jit(solution)/shard_map/ppermute | solution.py:27
  15.9 7.3 %collective-permute-start.6 = (s32[3,128]{1,0:T(4,128)S(1)}, s32[3,128]{1,0:T(4,128)S(1)}, u32[]{:S(2)}, u32[]{:S(2)}) collective-permute-start(s32[3,128]{1,0:T(4,128)S(1)} %get-tuple-element.79), channel_id=1, source_target_pairs={{0,1},{2,3},{4,5},{6,7},{8,9},{10,11},{12,13},{14,15},{16,17},{18,... | collective-permute-start | bytes 4616 | tf_op jit(solution)/shard_map/ppermute | solution.py:27
  24.2 10.0 %collective-permute-start.8 = (f32[3,128,256]{2,1,0:T(8,128)S(1)}, f32[3,128,256]{2,1,0:T(8,128)S(1)}, u32[]{:S(2)}, u32[]{:S(2)}) collective-permute-start(f32[3,128,256]{2,1,0:T(8,128)S(1)} %pad_maximum_fusion.3), channel_id=1, source_target_pairs={{0,30},{2,0},{4,2},{6,4},{8,6},{10,8},{12,10},{14,12},{16,14},{18,... | collective-permute-start | bytes 1179656 | tf_op jit(solution)/shard_map/ppermute | solution.py:21
  24.4 5.3 %collective-permute-start.2 = (f32[3,3,512]{2,1,0:T(4,128)S(1)}, f32[3,3,512]{2,1,0:T(4,128)S(1)}, u32[]{:S(2)}, u32[]{:S(2)}) collective-permute-start(f32[3,3,512]{2,1,0:T(4,128)S(1)} %get-tuple-element.67), channel_id=1, source_target_pairs={{0,1},{2,3},{4,5},{6,7},{8,9},{10,11},{12,13},{14,15},{16,17},{18,... | collective-permute-start | bytes 55304 | tf_op jit(solution)/shard_map/ppermute | solution.py:27
  27.1 5.7 %collective-permute-start.3 = (f32[3,3,512]{2,1,0:T(4,128)S(1)}, f32[3,3,512]{2,1,0:T(4,128)S(1)}, u32[]{:S(2)}, u32[]{:S(2)}) collective-permute-start(f32[3,3,512]{2,1,0:T(4,128)S(1)} %get-tuple-element.67), channel_id=1, source_target_pairs={{1,0},{3,2},{5,4},{7,6},{9,8},{11,10},{13,12},{15,14},{17,16},{19,... | collective-permute-start | bytes 55304 | tf_op jit(solution)/shard_map/ppermute | solution.py:27
  28.4 10.1 %collective-permute-start.9 = (f32[3,128,256]{2,1,0:T(8,128)S(1)}, f32[3,128,256]{2,1,0:T(8,128)}, u32[]{:S(2)}, u32[]{:S(2)}) collective-permute-start(f32[3,128,256]{2,1,0:T(8,128)S(1)} %pad_maximum_fusion.4), channel_id=1, source_target_pairs={{0,2},{2,4},{4,6},{6,8},{8,10},{10,12},{12,14},{14,16},{16,18},{18... | collective-permute-start | bytes 1179656 | tf_op jit(solution)/shard_map/ppermute | solution.py:21
  28.7 5.6 %copy-start.16 = (f32[1,1,512]{2,1,0:T(1,128)S(1)}, f32[1,1,512]{2,1,0:T(1,128)}, u32[]{:S(2)}) copy-start(f32[1,1,512]{2,1,0:T(1,128)} %param.8) | copy-start | bytes 6148
  28.7 5.6 %copy-start.12 = (f32[1,1,2,512]{3,2,1,0:T(2,128)S(1)}, f32[1,1,2,512]{3,2,1,0:T(2,128)}, u32[]{:S(2)}) copy-start(f32[1,1,2,512]{3,2,1,0:T(2,128)} %param.7) | copy-start | bytes 12292
  39.6 30.0 %collective-permute-start.10 = (f32[128,256]{1,0:T(8,128)S(1)}, f32[128,256]{1,0:T(8,128)S(1)}, u32[]{:S(2)}, u32[]{:S(2)}) collective-permute-start(f32[128,256]{1,0:T(8,128)S(1)} %get-tuple-element.38), channel_id=1, source_target_pairs={{1,0},{3,2},{5,4},{7,6},{9,8},{11,10},{13,12},{15,14},{17,16},{19,... | collective-permute-start | bytes 393224 | tf_op jit(solution)/shard_map/ppermute | solution.py:27
  40.9 28.7 %collective-permute-start.11 = (f32[128,256]{1,0:T(8,128)S(1)}, f32[128,256]{1,0:T(8,128)S(1)}, u32[]{:S(2)}, u32[]{:S(2)}) collective-permute-start(f32[128,256]{1,0:T(8,128)S(1)} %get-tuple-element.39), channel_id=1, source_target_pairs={{0,1},{2,3},{4,5},{6,7},{8,9},{10,11},{12,13},{14,15},{16,17},{18,... | collective-permute-start | bytes 393224 | tf_op jit(solution)/shard_map/ppermute | solution.py:27
  71.4 7.1 %collective-permute-start.12 = (f32[128,256]{1,0:T(8,128)S(1)}, f32[128,256]{1,0:T(8,128)S(1)}, u32[]{:S(2)}, u32[]{:S(2)}) collective-permute-start(f32[128,256]{1,0:T(8,128)S(1)} %get-tuple-element.15), channel_id=1, source_target_pairs={{0,2},{2,4},{4,6},{6,8},{8,10},{10,12},{12,14},{14,16},{16,18},{18... | collective-permute-start | bytes 393224 | tf_op jit(solution)/shard_map/ppermute | solution.py:21
  71.4 7.1 %collective-permute-start.13 = (f32[128,256]{1,0:T(8,128)S(1)}, f32[128,256]{1,0:T(8,128)S(1)}, u32[]{:S(2)}, u32[]{:S(2)}) collective-permute-start(f32[128,256]{1,0:T(8,128)S(1)} %get-tuple-element.15), channel_id=1, source_target_pairs={{0,30},{2,0},{4,2},{6,4},{8,6},{10,8},{12,10},{14,12},{16,14},{18,... | collective-permute-start | bytes 393224 | tf_op jit(solution)/shard_map/ppermute | solution.py:21
  78.5 6.6 %collective-permute-start.14 = (f32[3,128,256]{2,1,0:T(8,128)S(1)}, f32[3,128,256]{2,1,0:T(8,128)S(1)}, u32[]{:S(2)}, u32[]{:S(2)}) collective-permute-start(f32[3,128,256]{2,1,0:T(8,128)S(1)} %pad_maximum_fusion.5), channel_id=1, source_target_pairs={{0,1},{2,3},{4,5},{6,7},{8,9},{10,11},{12,13},{14,15},{16,17},{18,... | collective-permute-start | bytes 1179656 | tf_op jit(solution)/shard_map/ppermute | solution.py:27
  79.9 9.7 %collective-permute-start.15 = (f32[3,128,256]{2,1,0:T(8,128)S(1)}, f32[3,128,256]{2,1,0:T(8,128)S(1)}, u32[]{:S(2)}, u32[]{:S(2)}) collective-permute-start(f32[3,128,256]{2,1,0:T(8,128)S(1)} %pad_maximum_fusion.5), channel_id=1, source_target_pairs={{1,0},{3,2},{5,4},{7,6},{9,8},{11,10},{13,12},{15,14},{17,16},{19,... | collective-permute-start | bytes 1179656 | tf_op jit(solution)/shard_map/ppermute | solution.py:27
  90.1 12.7 %copy-start.6 = (f32[512,256]{1,0:T(8,128)}, f32[512,256]{1,0:T(8,128)S(1)}, u32[]{:S(2)}) copy-start(f32[512,256]{1,0:T(8,128)S(1)} %convolution_add_fusion.5.right_ref.left_ref) | copy-start | bytes 1572868
  90.2 11.5 %collective-permute-start.16 = (f32[512,256]{1,0:T(8,128)S(1)}, f32[512,256]{1,0:T(8,128)S(1)}, u32[]{:S(2)}, u32[]{:S(2)}) collective-permute-start(f32[512,256]{1,0:T(8,128)S(1)} %convolution_add_fusion.5.right_ref.left_ref), channel_id=1, source_target_pairs={{0,2},{2,4},{4,6},{6,8},{8,10},{10,12},{12,14},{14,16},{16,18},{18... | collective-permute-start | bytes 1572872 | tf_op jit(solution)/shard_map/ppermute | solution.py:21
  90.2 11.4 %collective-permute-start.17 = (f32[512,256]{1,0:T(8,128)S(1)}, f32[512,256]{1,0:T(8,128)S(1)}, u32[]{:S(2)}, u32[]{:S(2)}) collective-permute-start(f32[512,256]{1,0:T(8,128)S(1)} %convolution_add_fusion.5.right_ref.left_ref), channel_id=1, source_target_pairs={{0,30},{2,0},{4,2},{6,4},{8,6},{10,8},{12,10},{14,12},{16,14},{18,... | collective-permute-start | bytes 1572872 | tf_op jit(solution)/shard_map/ppermute | solution.py:21
  102.9 53.1 %collective-permute-start.18 = (f32[3,512,256]{2,1,0:T(8,128)}, f32[3,512,256]{2,1,0:T(8,128)}, u32[]{:S(2)}, u32[]{:S(2)}) collective-permute-start(f32[3,512,256]{2,1,0:T(8,128)} %pad_maximum_fusion), channel_id=1, source_target_pairs={{0,1},{2,3},{4,5},{6,7},{8,9},{10,11},{12,13},{14,15},{16,17},{18,... | collective-permute-start | bytes 4718600 | tf_op jit(solution)/shard_map/ppermute | solution.py:27
  105.6 59.1 %collective-permute-start.19 = (f32[3,512,256]{2,1,0:T(8,128)}, f32[3,512,256]{2,1,0:T(8,128)}, u32[]{:S(2)}, u32[]{:S(2)}) collective-permute-start(f32[3,512,256]{2,1,0:T(8,128)} %pad_maximum_fusion), channel_id=1, source_target_pairs={{1,0},{3,2},{5,4},{7,6},{9,8},{11,10},{13,12},{15,14},{17,16},{19,... | collective-permute-start | bytes 4718600 | tf_op jit(solution)/shard_map/ppermute | solution.py:27
  167.7 3.0 copy-start.7
  170.7 13.6 %copy-start.14 = (f32[1,256]{1,0:T(1,128)S(1)}, f32[1,256]{1,0:T(1,128)}, u32[]{:S(2)}) copy-start(f32[1,256]{1,0:T(1,128)} %shard_map.60) | copy-start | bytes 3076
  170.7 14.3 %copy-start.5 = (f32[1,1,512,256]{3,2,1,0:T(8,128)S(1)}, f32[1,1,512,256]{3,2,1,0:T(8,128)}, u32[]{:S(2)}) copy-start(f32[1,1,512,256]{3,2,1,0:T(8,128)} %param.6) | copy-start | bytes 1572868
  186.1 23.4 %copy-start = (f32[512,256]{1,0:T(8,128)}, f32[512,256]{1,0:T(8,128)S(1)}, u32[]{:S(2)}) copy-start(f32[512,256]{1,0:T(8,128)S(1)} %multiply_subtract_fusion.1.left_ref) | copy-start | bytes 1572868
  188.7 7.6 %collective-permute-start.20 = (f32[3,128,256]{2,1,0:T(8,128)S(1)}, f32[3,128,256]{2,1,0:T(8,128)S(1)}, u32[]{:S(2)}, u32[]{:S(2)}) collective-permute-start(f32[3,128,256]{2,1,0:T(8,128)S(1)} %pad_maximum_fusion.6), channel_id=1, source_target_pairs={{0,30},{2,0},{4,2},{6,4},{8,6},{10,8},{12,10},{14,12},{16,14},{18,... | collective-permute-start | bytes 1179656 | tf_op jit(solution)/shard_map/ppermute | solution.py:21
  191.1 10.0 %collective-permute-start.21 = (f32[3,128,256]{2,1,0:T(8,128)S(1)}, f32[3,128,256]{2,1,0:T(8,128)S(1)}, u32[]{:S(2)}, u32[]{:S(2)}) collective-permute-start(f32[3,128,256]{2,1,0:T(8,128)S(1)} %pad_maximum_fusion.7), channel_id=1, source_target_pairs={{0,2},{2,4},{4,6},{6,8},{8,10},{10,12},{12,14},{14,16},{16,18},{18... | collective-permute-start | bytes 1179656 | tf_op jit(solution)/shard_map/ppermute | solution.py:21
  201.2 6.9 %collective-permute-start.22 = (f32[128,256]{1,0:T(8,128)S(1)}, f32[128,256]{1,0:T(8,128)S(1)}, u32[]{:S(2)}, u32[]{:S(2)}) collective-permute-start(f32[128,256]{1,0:T(8,128)S(1)} %get-tuple-element.27), channel_id=1, source_target_pairs={{1,0},{3,2},{5,4},{7,6},{9,8},{11,10},{13,12},{15,14},{17,16},{19,... | collective-permute-start | bytes 393224 | tf_op jit(solution)/shard_map/ppermute | solution.py:27
  202.5 7.1 %collective-permute-start.23 = (f32[128,256]{1,0:T(8,128)S(1)}, f32[128,256]{1,0:T(8,128)S(1)}, u32[]{:S(2)}, u32[]{:S(2)}) collective-permute-start(f32[128,256]{1,0:T(8,128)S(1)} %get-tuple-element.28), channel_id=1, source_target_pairs={{0,1},{2,3},{4,5},{6,7},{8,9},{10,11},{12,13},{14,15},{16,17},{18,... | collective-permute-start | bytes 393224 | tf_op jit(solution)/shard_map/ppermute | solution.py:27
  211.3 7.1 %collective-permute-start.24 = (f32[128,256]{1,0:T(8,128)S(1)}, f32[128,256]{1,0:T(8,128)S(1)}, u32[]{:S(2)}, u32[]{:S(2)}) collective-permute-start(f32[128,256]{1,0:T(8,128)S(1)} %get-tuple-element.13), channel_id=1, source_target_pairs={{0,2},{2,4},{4,6},{6,8},{8,10},{10,12},{12,14},{14,16},{16,18},{18... | collective-permute-start | bytes 393224 | tf_op jit(solution)/shard_map/ppermute | solution.py:21
  211.4 7.1 %collective-permute-start.25 = (f32[128,256]{1,0:T(8,128)S(1)}, f32[128,256]{1,0:T(8,128)S(1)}, u32[]{:S(2)}, u32[]{:S(2)}) collective-permute-start(f32[128,256]{1,0:T(8,128)S(1)} %get-tuple-element.13), channel_id=1, source_target_pairs={{0,30},{2,0},{4,2},{6,4},{8,6},{10,8},{12,10},{14,12},{16,14},{18,... | collective-permute-start | bytes 393224 | tf_op jit(solution)/shard_map/ppermute | solution.py:21
  218.5 11.2 %collective-permute-start.26 = (f32[3,128,256]{2,1,0:T(8,128)S(1)}, f32[3,128,256]{2,1,0:T(8,128)S(1)}, u32[]{:S(2)}, u32[]{:S(2)}) collective-permute-start(f32[3,128,256]{2,1,0:T(8,128)S(1)} %pad_maximum_fusion.8), channel_id=1, source_target_pairs={{0,1},{2,3},{4,5},{6,7},{8,9},{10,11},{12,13},{14,15},{16,17},{18,... | collective-permute-start | bytes 1179656 | tf_op jit(solution)/shard_map/ppermute | solution.py:27
  222.9 11.0 %collective-permute-start.27 = (f32[3,128,256]{2,1,0:T(8,128)S(1)}, f32[3,128,256]{2,1,0:T(8,128)S(1)}, u32[]{:S(2)}, u32[]{:S(2)}) collective-permute-start(f32[3,128,256]{2,1,0:T(8,128)S(1)} %pad_maximum_fusion.8), channel_id=1, source_target_pairs={{1,0},{3,2},{5,4},{7,6},{9,8},{11,10},{13,12},{15,14},{17,16},{19,... | collective-permute-start | bytes 1179656 | tf_op jit(solution)/shard_map/ppermute | solution.py:27
  233.9 11.5 %copy-start.8 = (f32[512,256]{1,0:T(8,128)S(1)}, f32[512,256]{1,0:T(8,128)}, u32[]{:S(2)}) copy-start(f32[512,256]{1,0:T(8,128)} %copy-done.6) | copy-start | bytes 1572868
  246.5 57.5 %copy-start.9 = (f32[512,256]{1,0:T(8,128)}, f32[512,256]{1,0:T(8,128)S(1)}, u32[]{:S(2)}) copy-start(f32[512,256]{1,0:T(8,128)S(1)} %multiply_add_fusion.1.left_ref) | copy-start | bytes 1572868
  246.5 11.5 %collective-permute-start.28 = (f32[512,256]{1,0:T(8,128)S(1)}, f32[512,256]{1,0:T(8,128)S(1)}, u32[]{:S(2)}, u32[]{:S(2)}) collective-permute-start(f32[512,256]{1,0:T(8,128)S(1)} %multiply_add_fusion.1.left_ref), channel_id=1, source_target_pairs={{0,2},{2,4},{4,6},{6,8},{8,10},{10,12},{12,14},{14,16},{16,18},{18... | collective-permute-start | bytes 1572872 | tf_op jit(solution)/shard_map/ppermute | solution.py:21
  246.7 11.3 %collective-permute-start.29 = (f32[512,256]{1,0:T(8,128)S(1)}, f32[512,256]{1,0:T(8,128)S(1)}, u32[]{:S(2)}, u32[]{:S(2)}) collective-permute-start(f32[512,256]{1,0:T(8,128)S(1)} %multiply_add_fusion.1.left_ref), channel_id=1, source_target_pairs={{0,30},{2,0},{4,2},{6,4},{8,6},{10,8},{12,10},{14,12},{16,14},{18,... | collective-permute-start | bytes 1572872 | tf_op jit(solution)/shard_map/ppermute | solution.py:21
  258.1 36.4 %collective-permute-start.30 = (f32[3,512,256]{2,1,0:T(8,128)S(1)}, f32[3,512,256]{2,1,0:T(8,128)S(1)}, u32[]{:S(2)}, u32[]{:S(2)}) collective-permute-start(f32[3,512,256]{2,1,0:T(8,128)S(1)} %pad_maximum_fusion.1), channel_id=1, source_target_pairs={{0,1},{2,3},{4,5},{6,7},{8,9},{10,11},{12,13},{14,15},{16,17},{18,... | collective-permute-start | bytes 4718600 | tf_op jit(solution)/shard_map/ppermute | solution.py:27
  262.4 37.7 %collective-permute-start.31 = (f32[3,512,256]{2,1,0:T(8,128)S(1)}, f32[3,512,256]{2,1,0:T(8,128)S(1)}, u32[]{:S(2)}, u32[]{:S(2)}) collective-permute-start(f32[3,512,256]{2,1,0:T(8,128)S(1)} %pad_maximum_fusion.1), channel_id=1, source_target_pairs={{1,0},{3,2},{5,4},{7,6},{9,8},{11,10},{13,12},{15,14},{17,16},{19,... | collective-permute-start | bytes 4718600 | tf_op jit(solution)/shard_map/ppermute | solution.py:27
  304.0 16.9 %copy-start.13 = (f32[1,256]{1,0:T(1,128)S(1)}, f32[1,256]{1,0:T(1,128)}, u32[]{:S(2)}) copy-start(f32[1,256]{1,0:T(1,128)} %shard_map.62) | copy-start | bytes 3076
  304.0 17.6 %copy-start.1 = (f32[512,256]{1,0:T(8,128)S(1)}, f32[512,256]{1,0:T(8,128)}, u32[]{:S(2)}) copy-start(f32[512,256]{1,0:T(8,128)} %copy-done) | copy-start | bytes 1572868
  322.8 24.9 %copy-start.2 = (f32[512,256]{1,0:T(8,128)}, f32[512,256]{1,0:T(8,128)S(1)}, u32[]{:S(2)}) copy-start(f32[512,256]{1,0:T(8,128)S(1)} %multiply_subtract_fusion.left_ref) | copy-start | bytes 1572868
  325.3 9.1 %collective-permute-start.32 = (f32[3,128,256]{2,1,0:T(8,128)S(1)}, f32[3,128,256]{2,1,0:T(8,128)S(1)}, u32[]{:S(2)}, u32[]{:S(2)}) collective-permute-start(f32[3,128,256]{2,1,0:T(8,128)S(1)} %pad_maximum_fusion.9), channel_id=1, source_target_pairs={{0,30},{2,0},{4,2},{6,4},{8,6},{10,8},{12,10},{14,12},{16,14},{18,... | collective-permute-start | bytes 1179656 | tf_op jit(solution)/shard_map/ppermute | solution.py:21
  329.2 10.0 %collective-permute-start.33 = (f32[3,128,256]{2,1,0:T(8,128)S(1)}, f32[3,128,256]{2,1,0:T(8,128)S(1)}, u32[]{:S(2)}, u32[]{:S(2)}) collective-permute-start(f32[3,128,256]{2,1,0:T(8,128)S(1)} %pad_maximum_fusion.10), channel_id=1, source_target_pairs={{0,2},{2,4},{4,6},{6,8},{8,10},{10,12},{12,14},{14,16},{16,18},{18... | collective-permute-start | bytes 1179656 | tf_op jit(solution)/shard_map/ppermute | solution.py:21
  339.3 6.9 %collective-permute-start.34 = (f32[128,256]{1,0:T(8,128)S(1)}, f32[128,256]{1,0:T(8,128)S(1)}, u32[]{:S(2)}, u32[]{:S(2)}) collective-permute-start(f32[128,256]{1,0:T(8,128)S(1)} %get-tuple-element.16), channel_id=1, source_target_pairs={{1,0},{3,2},{5,4},{7,6},{9,8},{11,10},{13,12},{15,14},{17,16},{19,... | collective-permute-start | bytes 393224 | tf_op jit(solution)/shard_map/ppermute | solution.py:27
  340.6 7.1 %collective-permute-start.35 = (f32[128,256]{1,0:T(8,128)S(1)}, f32[128,256]{1,0:T(8,128)S(1)}, u32[]{:S(2)}, u32[]{:S(2)}) collective-permute-start(f32[128,256]{1,0:T(8,128)S(1)} %get-tuple-element.17), channel_id=1, source_target_pairs={{0,1},{2,3},{4,5},{6,7},{8,9},{10,11},{12,13},{14,15},{16,17},{18,... | collective-permute-start | bytes 393224 | tf_op jit(solution)/shard_map/ppermute | solution.py:27
  349.4 7.1 %collective-permute-start.36 = (f32[128,256]{1,0:T(8,128)S(1)}, f32[128,256]{1,0:T(8,128)S(1)}, u32[]{:S(2)}, u32[]{:S(2)}) collective-permute-start(f32[128,256]{1,0:T(8,128)S(1)} %get-tuple-element.11), channel_id=1, source_target_pairs={{0,2},{2,4},{4,6},{6,8},{8,10},{10,12},{12,14},{14,16},{16,18},{18... | collective-permute-start | bytes 393224 | tf_op jit(solution)/shard_map/ppermute | solution.py:21
  349.5 7.1 %collective-permute-start.37 = (f32[128,256]{1,0:T(8,128)S(1)}, f32[128,256]{1,0:T(8,128)S(1)}, u32[]{:S(2)}, u32[]{:S(2)}) collective-permute-start(f32[128,256]{1,0:T(8,128)S(1)} %get-tuple-element.11), channel_id=1, source_target_pairs={{0,30},{2,0},{4,2},{6,4},{8,6},{10,8},{12,10},{14,12},{16,14},{18,... | collective-permute-start | bytes 393224 | tf_op jit(solution)/shard_map/ppermute | solution.py:21
  356.6 9.8 %collective-permute-start.38 = (f32[3,128,256]{2,1,0:T(8,128)S(1)}, f32[3,128,256]{2,1,0:T(8,128)S(1)}, u32[]{:S(2)}, u32[]{:S(2)}) collective-permute-start(f32[3,128,256]{2,1,0:T(8,128)S(1)} %pad_maximum_fusion.11), channel_id=1, source_target_pairs={{0,1},{2,3},{4,5},{6,7},{8,9},{10,11},{12,13},{14,15},{16,17},{18,... | collective-permute-start | bytes 1179656 | tf_op jit(solution)/shard_map/ppermute | solution.py:27
  361.0 9.7 %collective-permute-start.39 = (f32[3,128,256]{2,1,0:T(8,128)S(1)}, f32[3,128,256]{2,1,0:T(8,128)S(1)}, u32[]{:S(2)}, u32[]{:S(2)}) collective-permute-start(f32[3,128,256]{2,1,0:T(8,128)S(1)} %pad_maximum_fusion.11), channel_id=1, source_target_pairs={{1,0},{3,2},{5,4},{7,6},{9,8},{11,10},{13,12},{15,14},{17,16},{19,... | collective-permute-start | bytes 1179656 | tf_op jit(solution)/shard_map/ppermute | solution.py:27
  370.7 11.5 %copy-start.10 = (f32[512,256]{1,0:T(8,128)S(1)}, f32[512,256]{1,0:T(8,128)}, u32[]{:S(2)}) copy-start(f32[512,256]{1,0:T(8,128)} %copy-done.9) | copy-start | bytes 1572868
  383.3 57.5 %copy-start.11 = (f32[512,256]{1,0:T(8,128)}, f32[512,256]{1,0:T(8,128)S(1)}, u32[]{:S(2)}) copy-start(f32[512,256]{1,0:T(8,128)S(1)} %multiply_add_fusion.left_ref) | copy-start | bytes 1572868
  383.3 11.5 %collective-permute-start.40 = (f32[512,256]{1,0:T(8,128)S(1)}, f32[512,256]{1,0:T(8,128)S(1)}, u32[]{:S(2)}, u32[]{:S(2)}) collective-permute-start(f32[512,256]{1,0:T(8,128)S(1)} %multiply_add_fusion.left_ref), channel_id=1, source_target_pairs={{0,2},{2,4},{4,6},{6,8},{8,10},{10,12},{12,14},{14,16},{16,18},{18... | collective-permute-start | bytes 1572872 | tf_op jit(solution)/shard_map/ppermute | solution.py:21
  383.5 11.3 %collective-permute-start.41 = (f32[512,256]{1,0:T(8,128)S(1)}, f32[512,256]{1,0:T(8,128)S(1)}, u32[]{:S(2)}, u32[]{:S(2)}) collective-permute-start(f32[512,256]{1,0:T(8,128)S(1)} %multiply_add_fusion.left_ref), channel_id=1, source_target_pairs={{0,30},{2,0},{4,2},{6,4},{8,6},{10,8},{12,10},{14,12},{16,14},{18,... | collective-permute-start | bytes 1572872 | tf_op jit(solution)/shard_map/ppermute | solution.py:21
  394.9 36.4 %collective-permute-start.42 = (f32[3,512,256]{2,1,0:T(8,128)S(1)}, f32[3,512,256]{2,1,0:T(8,128)S(1)}, u32[]{:S(2)}, u32[]{:S(2)}) collective-permute-start(f32[3,512,256]{2,1,0:T(8,128)S(1)} %pad_maximum_fusion.2), channel_id=1, source_target_pairs={{0,1},{2,3},{4,5},{6,7},{8,9},{10,11},{12,13},{14,15},{16,17},{18,... | collective-permute-start | bytes 4718600 | tf_op jit(solution)/shard_map/ppermute | solution.py:27
  399.2 37.7 %collective-permute-start.43 = (f32[3,512,256]{2,1,0:T(8,128)S(1)}, f32[3,512,256]{2,1,0:T(8,128)S(1)}, u32[]{:S(2)}, u32[]{:S(2)}) collective-permute-start(f32[3,512,256]{2,1,0:T(8,128)S(1)} %pad_maximum_fusion.2), channel_id=1, source_target_pairs={{1,0},{3,2},{5,4},{7,6},{9,8},{11,10},{13,12},{15,14},{17,16},{19,... | collective-permute-start | bytes 4718600 | tf_op jit(solution)/shard_map/ppermute | solution.py:27
  440.8 17.4 %copy-start.15 = (f32[1,256]{1,0:T(1,128)S(1)}, f32[1,256]{1,0:T(1,128)}, u32[]{:S(2)}) copy-start(f32[1,256]{1,0:T(1,128)} %shard_map.64) | copy-start | bytes 3076
  440.8 18.1 %copy-start.3 = (f32[512,256]{1,0:T(8,128)S(1)}, f32[512,256]{1,0:T(8,128)}, u32[]{:S(2)}) copy-start(f32[512,256]{1,0:T(8,128)} %copy-done.2) | copy-start | bytes 1572868
